TPU v7x, 32 devices: a whole 2x2x4 slice. The times are simulated.
32 devices in a mesh: flow: 16 (over z, y, x), group: 2 (over core).
Axes of the slice: x: 2, y: 2, z: 4, core: 2. Of those that a mesh axis runs over, the one named last changes fastest.
Arguments:
- density: float32 [64, 32, 256], P('flow', 'group'), may hold values from 0.8 to 1.2
- velocity: float32 [3, 64, 32, 256], P(None, 'flow', 'group'), may hold values from -0.5 to 0.5
- pressure: float32 [64, 32, 256], P('flow', 'group'), may hold values from 0.7 to 1.3
- wave_state: float32 [4, 8, 8, 8, 4096], P(None, None, None, None, ('flow', 'group')), may hold values from -1.8 to 1.8
- tables: float32 [4, 512, 512], replicated, may hold values from -0.75 to 0.75
- margin_element: int32 [32, 64], P(('flow', 'group')), may hold values from 0 to 4095, as said below
- margin_block: int32 [32, 64], P(('flow', 'group')), may hold values from 0 to 31
- margin_table: int32 [32, 64], P(('flow', 'group')), may hold values from 0 to 3
Outputs:
- flow_state: float32 [5, 64, 32, 256], P(None, 'flow', 'group')
- wave_out: float32 [4, 8, 8, 8, 4096], P(None, None, None, None, ('flow', 'group'))
- forcing: float32 [3, 8, 8, 8, 4096], P(None, None, None, None, ('flow', 'group'))
Inputs may be any that keep to these rules, and one draw needn't show every extreme that they name: `margin_element`: global element ids; element e belongs to the device at position e // 128 along flow then group. In every device's row at most 4 entries name elements of one owner, and some owner receives exactly 4 entries from it.
All inputs are finite; a program needn't handle non-finite values.
Results may differ from a plain program's by a relative error of at most 0.0003.
Values sent between devices are 32-bit elements; how exact they have to be, the bound alone decides.
A program may use at most 128 MiB of HBM per device.

v0:
```python
import jax
import jax.numpy as jnp
import numpy as np
from jax import lax
from jax.experimental import pallas as pl
from jax.experimental.pallas import tpu as pltpu
from jax.sharding import PartitionSpec as P

EZ = 16
CAP = 4
STEPS = 2

GAMMA = 1.4
DT_FLOW = 0.08
ACOUSTIC_STEP = 0.01
F32, BF16 = jnp.float32, jnp.bfloat16
KEEP = (0.0, 0.75, 1.0 / 3.0)
GAIN = (1.0, 0.25, 2.0 / 3.0)


def legendre_pair(quadrature_nodes, degree):
    previous = np.ones(quadrature_nodes.shape[0])
    current = quadrature_nodes * 1.0
    for order in range(2, degree + 1):
        previous, current = (
            current,
            ((2 * order - 1) * quadrature_nodes * current - (order - 1) * previous) / order,
        )
    return (previous, current)


def lobatto(point_count):
    degree = point_count - 1
    quadrature_nodes = -np.cos(np.pi * np.arange(point_count) / degree)
    for sweep in range(60):
        previous, current = legendre_pair(quadrature_nodes, degree)
        quadrature_nodes = quadrature_nodes - (quadrature_nodes * current - previous) / (
            point_count * current
        )
    previous, values = legendre_pair(quadrature_nodes, degree)
    quadrature_weights = 2.0 / (degree * (degree + 1) * values**2)
    identity = np.eye(point_count)
    differ = quadrature_nodes[:, None] - quadrature_nodes[None, :] + identity
    matrix = values[:, None] / values[None, :] / differ * (1.0 - identity)
    matrix[0, 0] = -degree * (degree + 1) / 4.0
    matrix[-1, -1] = degree * (degree + 1) / 4.0
    return (matrix, float(quadrature_weights[0]))


def iota(shape, axis):
    return lax.broadcasted_iota(jnp.int32, shape, axis)


def split(value):
    high = value.astype(BF16)
    return high, (value - high.astype(F32)).astype(BF16)


def dot(a, b):
    return jnp.dot(a, b, preferred_element_type=F32)


def primitive(state):
    inverse = 1.0 / state[0]
    vel = [state[1 + d] * inverse for d in range(3)]
    square = vel[0] * vel[0] + vel[1] * vel[1] + vel[2] * vel[2]
    pressure = (GAMMA - 1.0) * (state[4] - 0.5 * state[0] * square)
    return vel, pressure, jnp.sqrt(GAMMA * pressure * inverse)


def flux_of(state, prim, d):
    vel, pressure, sound = prim
    normal = vel[d]
    parts = [state[0] * normal]
    for c in range(3):
        product = state[1 + c] * normal
        parts.append(product + pressure if c == d else product)
    parts.append((state[4] + pressure) * normal)
    return parts, jnp.abs(normal) + sound


def face(left, right, left_flux, right_flux, left_speed, right_speed):
    speed = jnp.maximum(left_speed, right_speed)
    return [
        0.5 * (left_flux[c] + right_flux[c]) - 0.5 * speed * (right[c] - left[c])
        for c in range(5)
    ]


def along(cell, prim, d, axis):
    size = cell[0].shape[axis]
    flux, speed = flux_of(cell, prim, d)
    back = lambda v: pltpu.roll(v, size - 1, axis)
    upper = face(
        cell, [back(v) for v in cell], flux, [back(v) for v in flux], speed, back(speed)
    )
    return [upper[c] - pltpu.roll(upper[c], 1, axis) for c in range(5)]


def tall_of(own, above, below):
    row = iota(above.shape, 0)
    return jnp.concatenate([own, jnp.where(row < above.shape[0] // 2, above, below)], axis=0)


def flow_stage(src, above, below, finish, before, after):
    planes, rows = src.shape[1] - 2, src.shape[2]

    def load(p):
        return [src[c, p] for c in range(5)]

    def x_side(p):
        cell = load(p)
        flux, speed = flux_of(cell, primitive(cell), 0)
        return cell, flux, speed

    def x_face(p):
        left, right = x_side(p), x_side(p + 1)
        return face(left[0], right[0], left[1], right[1], left[2], right[2])

    def body(p, lower):
        before(p)
        upper = x_face(p + 1)
        tall = [tall_of(src[c, p + 1], above[c, p], below[c, p]) for c in range(5)]
        prim = primitive(tall)
        dy = along(tall, prim, 1, 0)
        cell = [v[:rows] for v in tall]
        prim = ([v[:rows] for v in prim[0]], prim[1][:rows], prim[2][:rows])
        dz = along(cell, prim, 2, 1)
        for c in range(5):
            rate = -(upper[c] - lower[c]) - dy[c][:rows] - dz[c]
            finish(p, c, cell[c] + DT_FLOW * rate)
        after(p)
        return tuple(upper)

    lax.fori_loop(0, planes, body, tuple(x_face(0)))


def lamb(src, above, below, out):
    planes, rows, columns = src.shape[1] - 2, src.shape[2], src.shape[3]

    def body(p, _):
        density = tall_of(src[0, p + 1], above[0, p], below[0, p])
        inverse = 1.0 / density
        tall = [
            tall_of(src[1 + d, p + 1], above[1 + d, p], below[1 + d, p]) * inverse
            for d in range(3)
        ]
        size = tall[0].shape[0]
        slope_y = [
            0.5 * (pltpu.roll(v, size - 1, 0) - pltpu.roll(v, 1, 0))[:rows] for v in tall
        ]
        vel = [v[:rows] for v in tall]
        slope_z = [0.5 * (pltpu.roll(v, columns - 1, 1) - pltpu.roll(v, 1, 1)) for v in vel]
        after, before = 1.0 / src[0, p + 2], 1.0 / src[0, p]
        slope_x = [
            0.5 * (src[1 + d, p + 2] * after - src[1 + d, p] * before) for d in range(3)
        ]
        curl_x = slope_y[2] - slope_z[1]
        curl_y = slope_z[0] - slope_x[2]
        curl_z = slope_x[1] - slope_y[0]
        result = [
            curl_y * vel[2] - curl_z * vel[1],
            curl_z * vel[0] - curl_x * vel[2],
            curl_x * vel[1] - curl_y * vel[0],
        ]
        for d in range(3):
            for q in range(out.shape[2]):
                out[d, p, q] = result[d][:, q * 128 : (q + 1) * 128]
        return 0

    lax.fori_loop(0, planes, body, 0)


def split_tables(tables, high, low):
    count, depth, _ = tables.shape
    step = 64

    def body(i, _):
        t = i // (depth // step)
        at = pl.ds(pl.multiple_of((i % (depth // step)) * step, step), step)
        h, l = split(tables[t, at, :])
        high[t, at, :] = h
        low[t, at, :] = l
        return 0

    lax.fori_loop(0, count * (depth // step), body, 0)


def rows_of_slots(source, high, low, pick, mapped_high, mapped_low, send):
    _, planes, chunks, rows, width = source.shape
    columns = chunks * width
    table_count, depth, nodes = high.shape
    per = depth // columns
    strip = rows // per
    blocks = planes * strip
    half = 3 * nodes // 2
    pieces = []
    for y in range(3):
        for p in range(planes):
            pieces.append(
                jnp.concatenate(
                    [
                        source[y, p, q, pl.ds(r, strip, stride=per), :]
                        for r in range(per)
                        for q in range(chunks)
                    ],
                    axis=1,
                )
            )
    left_high, left_low = split(jnp.concatenate(pieces, axis=0))
    both = jnp.concatenate([left_high, left_low], axis=0)
    count = 3 * blocks

    def body(t, _):
        wide = dot(both, high[t])
        out = wide[:count] + wide[count:] + dot(left_high, low[t])
        for side in range(2):
            at = pl.ds(pl.multiple_of(side * table_count * blocks + t * blocks, blocks), blocks)
            for y in range(3):
                begin, end = max(y * nodes, side * half), min((y + 1) * nodes, (side + 1) * half)
                if begin < end:
                    value = out[y * blocks : (y + 1) * blocks, begin - y * nodes : end - y * nodes]
                    h, l = split(value)
                    mapped_high[at, begin - side * half : end - side * half] = h
                    mapped_low[at, begin - side * half : end - side * half] = l
        return 0

    lax.fori_loop(0, table_count, body, 0)
    send[...] = dot(pick[...], mapped_high[...]) + dot(pick[...], mapped_low[...])


def routes(element, block, table, blocks, table_count, local_count, devices, pick, label):
    entries = element.shape[1]
    shift = local_count.bit_length() - 1
    assert 1 << shift == local_count
    owner = lax.shift_right_logical(element, shift)
    local_index = element - lax.shift_left(owner, shift)
    column = table * blocks + block
    square = (entries, entries)
    row = jnp.broadcast_to(owner, square)
    turned = jnp.sum(jnp.where(iota(square, 0) == iota(square, 1), row, 0), axis=1, keepdims=True)
    earlier = (turned == row) & (iota(square, 0) < iota(square, 1))
    rank = jnp.sum(jnp.where(earlier, 1, 0), axis=0, keepdims=True)
    slot = owner * CAP + rank
    high = 2 * CAP
    lines = devices * high
    line = iota((lines, entries), 0)
    named = (line // high) * CAP + line % CAP
    hit = named == slot
    labels = jnp.sum(jnp.where(hit, local_index + 1, 0), axis=1, keepdims=True) - 1
    picked = jnp.sum(jnp.where(hit, column + 1, 0), axis=1, keepdims=True) - 1
    tiles = (devices, high, label.shape[2])
    spread = jnp.broadcast_to(labels, (lines, tiles[2])).reshape(tiles)
    label[...] = jnp.sum(
        jnp.where(iota(tiles, 1) == iota(tiles, 2), spread, 0), axis=1, keepdims=True
    )
    shape = pick.shape
    side = (iota(shape, 0) // CAP) % 2
    chosen = picked + side * (table_count * blocks)
    on = (iota(shape, 1) == chosen) & (picked >= 0)
    pick[...] = jnp.where(on, 1.0, 0.0).astype(BF16)


def place_of(label, place):
    devices, _, lanes = label.shape
    high = 2 * CAP
    shape = (devices * high, lanes)
    wide = jnp.broadcast_to(label[...], (devices, high, lanes)).reshape(shape)
    line, lane = iota(shape, 0), iota(shape, 1)
    named = jnp.sum(jnp.where(line % CAP == lane, wide, 0), axis=1, keepdims=True)
    side = (line // CAP) % 2
    hit = named == lane
    for s in range(2):
        place[:, s * lanes : (s + 1) * lanes] = jnp.where(hit & (side == s), 1.0, 0.0).astype(BF16)


def add_up(received, place, forcing):
    parts, lanes = forcing.shape[0] // 2, forcing.shape[-1]
    high, low = split(received[...].T)
    total = dot(high, place[...]) + dot(low, place[...])
    for s in range(2):
        forcing[s * parts : (s + 1) * parts] = total[:, s * lanes : (s + 1) * lanes].reshape(
            (parts,) + forcing.shape[1:]
        )


def halves(matrix):
    n = matrix.shape[0]
    turned = matrix[: n // 2, ::-1][:, : n // 2]
    own = matrix[: n // 2, : n // 2]
    return 0.5 * (own + turned), 0.5 * (own - turned)


def derive(values, even, odd):
    n = len(values)
    h = n // 2
    sums = [values[m] + values[n - 1 - m] for m in range(h)]
    gaps = [values[m] - values[n - 1 - m] for m in range(h)]
    out = [None] * n
    for a in range(h):
        alpha = sum(float(even[a, m]) * sums[m] for m in range(h))
        beta = sum(float(odd[a, m]) * gaps[m] for m in range(h))
        out[a] = beta + alpha
        out[n - 1 - a] = beta - alpha
    return out


def wave_main(start, cur, forcing, out, partial, edge, dcol, matrix, lift, stage, forced):
    keep, gain = KEEP[stage], GAIN[stage]
    n, lanes = cur.shape[1], cur.shape[-1]
    last = n - 1
    even, odd = halves(matrix)
    node = iota((n, lanes), 0)
    z = iota((n, lanes), 1) % EZ
    turn = lambda v, by: pltpu.roll(v, by % lanes, v.ndim - 1)

    def store(f, i, j, rate):
        value = gain * cur[f, i, j] + (gain * ACOUSTIC_STEP) * rate
        if keep:
            value = keep * start[f, i, j] + value
        out[f, i, j] = value

    def push(d, i, j):
        return forcing[d * n + i, j] if forced else 0.0

    def edges(i, _):
        p7, u7 = cur[0, i, :, last, :], cur[3, i, :, last, :]
        p0, u0 = cur[0, i, :, 0, :], cur[3, i, :, 0, :]
        plus, minus = u7 + p7, u0 - p0
        below = jnp.where(z == 0, turn(plus, 1 - EZ), turn(plus, 1))
        above = jnp.where(z == EZ - 1, turn(minus, EZ - 1), turn(minus, -1))
        edge[0, i] = lift * (below - (u0 + p0))
        edge[1, i] = lift * (above - (u7 - p7))
        return 0

    lax.fori_loop(0, n, edges, 0)

    def lines_i(j, _):
        d_u = derive([cur[1, i, j] for i in range(n)], even, odd)
        d_p = derive([cur[0, i, j] for i in range(n)], even, odd)
        for i in range(n):
            store(1, i, j, push(0, i, j) - d_p[i])
            rate_p, rate_w = d_u[i], 0.0
            for m in range(n):
                rate_p = rate_p + dcol[m] * cur[3, i, j, m : m + 1, :]
                rate_w = rate_w + dcol[m] * cur[0, i, j, m : m + 1, :]
            low = jnp.where(node == 0, edge[0, i, pl.ds(j, 1), :], 0.0)
            up = jnp.where(node == last, edge[1, i, pl.ds(j, 1), :], 0.0)
            partial[i, j] = (low - up) - rate_p
            store(3, i, j, push(2, i, j) + ((low + up) - rate_w))
        return 0

    lax.fori_loop(0, n, lines_i, 0)

    def lines_j(i, _):
        p = [cur[0, i, j] for j in range(n)]
        v = [cur[2, i, j] for j in range(n)]
        low = lift * (turn(v[last] + p[last], EZ) - (v[0] + p[0]))
        up = lift * (turn(v[0] - p[0], -EZ) - (v[last] - p[last]))
        d_v = derive(v, even, odd)
        d_p = derive(p, even, odd)
        for j in range(n):
            rate_p, rate_v = partial[i, j] - d_v[j], push(1, i, j) - d_p[j]
            if j == 0:
                rate_p, rate_v = rate_p + low, rate_v + low
            if j == last:
                rate_p, rate_v = rate_p - up, rate_v + up
            store(0, i, j, rate_p)
            store(2, i, j, rate_v)
        return 0

    lax.fori_loop(0, n, lines_j, 0)


def wave_force(out, forcing, stage):
    n = out.shape[1]
    scale = GAIN[stage] * ACOUSTIC_STEP

    def body(i, _):
        for d in range(3):
            out[1 + d, i] = out[1 + d, i] + scale * forcing[d * n + i]
        return 0

    lax.fori_loop(0, n, body, 0)


def wave_faces(cur, out, below, above, lift, stage):
    last = cur.shape[1] - 1
    scale = GAIN[stage] * ACOUSTIC_STEP * lift
    low = scale * (below[...] - (cur[1, 0] + cur[0, 0]))
    out[0, 0] = out[0, 0] + low
    out[1, 0] = out[1, 0] + low
    up = scale * (above[...] - (cur[1, last] - cur[0, last]))
    out[0, last] = out[0, last] - up
    out[1, last] = out[1, last] + up


def all_kernel(
    sizes, den_hbm, vel_hbm, pre_hbm, wave_hbm, tables_hbm, element, block, table,
    fields_out, wave_out, forcing_out,
    den, vel, pre, wave0, tables, high, low, X0, X1, X2, X3, X4, X5,
    A0, A1, A2, A3, A4, A5, B0, B1, B2, B3, B4, B5, S, pick, label, label_in, place,
    mapped_high, mapped_low, send, recv, forcing1, partial, edge, dcol, V, FS, FR,
    local_sem, x_send, x_recv, y_send, y_recv, w_send, w_recv, l_send, l_recv, a_send, a_recv,
):
    flows, groups, local_count = sizes
    devices = flows * groups
    planes, rows, columns = den.shape
    f, g = lax.axis_index("flow"), lax.axis_index("group")
    me = f * groups + g
    at = lambda k: (k // groups, k % groups)
    matrix, end_weight = lobatto(wave0.shape[1])
    lift = 0.5 / end_weight
    n = wave0.shape[1]

    loads = [
        pltpu.make_async_copy(a, b, local_sem.at[i])
        for i, (a, b) in enumerate(
            [(den_hbm, den), (vel_hbm, vel), (pre_hbm, pre), (wave_hbm, wave0), (tables_hbm, tables)]
        )
    ]
    for c in loads:
        c.start()
    barrier = pltpu.get_barrier_semaphore()

    def greet(d, _):
        pl.semaphore_signal(
            barrier, inc=1, device_id=at((me + d) % devices), device_id_type=pl.DeviceIdType.MESH
        )
        return 0

    lax.fori_loop(1, devices, greet, 0)

    pending = []

    def remote(src, dst, ssem, rsem, device):
        c = pltpu.make_async_remote_copy(
            src_ref=src, dst_ref=dst, send_sem=ssem, recv_sem=rsem,
            device_id=device, device_id_type=pl.DeviceIdType.MESH,
        )
        c.start()
        pending.append(c)
        return c

    X = [X0, X1, X2, X3, X4, X5]
    A, B = [A0, A1, A2, A3, A4, A5], [B0, B1, B2, B3, B4, B5]
    r8 = A0.shape[2]
    up_g, down_g = (f, (g + 1) % groups), (f, (g + groups - 1) % groups)
    up_f, down_f = ((f + 1) % flows, g), ((f + flows - 1) % flows, g)

    def y_copies(s, p):
        return [
            pltpu.make_async_remote_copy(
                src_ref=X[s].at[:, p + 1, band], dst_ref=ghost[s].at[:, p],
                send_sem=y_send.at[s, way, p], recv_sem=y_recv.at[s, way, p],
                device_id=device, device_id_type=pl.DeviceIdType.MESH,
            )
            for way, (band, ghost, device) in enumerate(
                [(slice(0, r8), A, down_g), (slice(rows - r8, rows), B, up_g)]
            )
        ]

    def send_y(s, p):
        for c in y_copies(s, p):
            c.start()

    def wait_y(s, p):
        for c in y_copies(s, p):
            c.wait_recv()

    def over(begin, end, do):
        def body(p, _):
            do(p)
            return 0
        lax.fori_loop(begin, end, body, 0)

    def send_x(s, i, low, low_to, high, high_to):
        return [
            remote(X[s].at[:, low], X[s].at[:, low_to], x_send.at[s, i], x_recv.at[s, i], down_f),
            remote(X[s].at[:, high], X[s].at[:, high_to], x_send.at[s, i + 1], x_recv.at[s, i + 1], up_f),
        ]

    def send_halos(s):
        return send_x(s, 0, slice(1, 2), slice(planes + 1, planes + 2), slice(planes, planes + 1), slice(0, 1))

    def send_faces(s, cur):
        last = n - 1
        FS[s, 0] = cur[1, last] + cur[0, last]
        FS[s, 1] = cur[1, 0] - cur[0, 0]
        return [
            remote(FS.at[s, 0], FR.at[s, 0], w_send.at[s, 0], w_recv.at[s, 0], at((me + 1) % devices)),
            remote(FS.at[s, 1], FR.at[s, 1], w_send.at[s, 1], w_recv.at[s, 1], at((me + devices - 1) % devices)),
        ]

    def arrive(copies):
        for c in copies:
            c.wait_recv()

    high_rows = 2 * CAP

    def slot_copy(src, dst, ssem, rsem, peer, owner):
        size = src.shape[0] // devices
        block_at = lambda k: pl.ds(pl.multiple_of(k * size, size), size)
        return pltpu.make_async_remote_copy(
            src_ref=src.at[block_at(peer)], dst_ref=dst.at[block_at(owner)],
            send_sem=ssem, recv_sem=rsem,
            device_id=at(peer), device_id_type=pl.DeviceIdType.MESH,
        )

    stride = 11 if np.gcd(11, devices) == 1 else 1

    def exchange(src, dst, ssem, rsem, begin, end):
        def body(k, _):
            slot_copy(src, dst, ssem, rsem, (me + k * stride) % devices, me).start()
            return 0
        lax.fori_loop(begin, end, body, 0)

    def keep_own(src, dst):
        size = src.shape[0] // devices
        mine = pl.ds(pl.multiple_of(me * size, size), size)
        dst[mine] = src[mine]

    def all_blocks(src, dst, ssem, rsem):
        others = pl.ds(0, (devices - 1) * (src.shape[0] // devices))
        return pltpu.make_async_remote_copy(
            src_ref=src.at[others], dst_ref=dst.at[others], send_sem=ssem, recv_sem=rsem,
            device_id=at((me + 1) % devices), device_id_type=pl.DeviceIdType.MESH,
        )

    def settle(*refs):
        all_blocks(*refs).wait_recv()

    def drain(*refs):
        all_blocks(*refs).wait_send()

    for c in loads[:3]:
        c.wait()

    deep = 4
    assert planes >= deep

    def conserve(p, _):
        r = den[p]
        v = [vel[d, p] for d in range(3)]
        X0[0, p + deep] = r
        for d in range(3):
            X0[1 + d, p + deep] = r * v[d]
        square = v[0] * v[0] + v[1] * v[1] + v[2] * v[2]
        X0[4, p + deep] = pre[p] / (GAMMA - 1.0) + 0.5 * r * square
        return 0

    lax.fori_loop(0, planes, conserve, 0)
    pl.semaphore_wait(barrier, devices - 1)
    near = send_x(
        0, 0, slice(deep, deep + 1), slice(deep + planes, deep + planes + 1),
        slice(deep + planes - 1, deep + planes), slice(deep - 1, deep),
    )
    over(deep - 1, deep - 1 + planes, lambda p: send_y(0, p))
    far = send_x(
        0, 2, slice(deep + 1, 2 * deep), slice(deep + planes + 1, 2 * deep + planes),
        slice(planes, deep + planes - 1), slice(0, deep - 1),
    )
    loads[3].wait()
    waves = send_faces(0, wave0)
    blocks = planes * rows * columns // tables.shape[1]
    routes(element[...], block[...], table[...], blocks, tables.shape[0], local_count, devices, pick, label)
    exchange(label, label_in, l_send, l_recv, 1, devices)
    keep_own(label, label_in)
    row = iota((n, dcol.shape[-1]), 0)
    for m in range(n):
        tile = jnp.zeros((n, dcol.shape[-1]), F32)
        for k in range(n):
            tile = jnp.where(row == k, float(matrix[k, m]), tile)
        dcol[m] = tile
    loads[4].wait()
    split_tables(tables, high, low)

    forcings = [forcing1, forcing_out]
    def flow_part(s):
        step, stage = s // 3, s % 3
        base = 3 * step
        lag = 1 if s >= 3 else 0
        total = X[s].shape[1] - 2

        def finish(p, c, value):
            if stage:
                value = KEEP[stage] * X[base][c, p + (stage + 1 if s < 3 else 1)] + GAIN[stage] * value
            if s == 3 * STEPS - 1:
                fields_out[c, p] = value
            else:
                X[s + 1][c, p + lag] = value

        def before(p):
            if s not in (0, 3):
                wait_y(s, p)

        def after(p):
            if s == 3 * STEPS - 1:
                return
            first = 1 if lag else 2

            @pl.when((p >= first) & (p - first < X[s + 1].shape[1] - 2))
            def _():
                send_y(s + 1, p - first)

        flow_stage(X[s], A[s], B[s], finish, before, after)
        if lag and s < 3 * STEPS - 1:
            send_y(s + 1, total - 1)

    def project(step):
        rows_of_slots(S, high, low, pick, mapped_high, mapped_low, send.at[step])
        keep_own(send.at[step], recv.at[step])

    def issue(step, begin, end):
        cut = lambda t: 1 + int(round(t * (devices - 1)))
        exchange(send.at[step], recv.at[step], a_send.at[step], a_recv.at[step], cut(begin), cut(end))

    curs = [wave0] + [V.at[i] for i in range(5)] + [wave_out]

    def main(s, forced):
        step, stage = s // 3, s % 3
        wave_main(curs[3 * step], curs[s], forcings[step], curs[s + 1], partial, edge, dcol,
                  matrix, lift, stage, forced)

    def finish_wave(s, copies):
        arrive(copies)
        wave_faces(curs[s], curs[s + 1], FR.at[s, 0], FR.at[s, 1], lift, s % 3)

    main(0, False)
    arrive(near)
    over(deep - 1, deep - 1 + planes, lambda p: wait_y(0, p))
    mid, own = pl.ds(deep - 1, planes + 2), pl.ds(deep - 1, planes)
    lamb(X0.at[:, mid], A0.at[:, own], B0.at[:, own], S)
    project(0)
    issue(0, 0.0, 1.0)
    arrive(far)
    for part in ((0, deep - 1), (deep - 1 + planes, 2 * deep + planes - 2)):
        over(*part, lambda p: send_y(0, p))
    for part in ((0, deep - 1), (deep - 1 + planes, 2 * deep + planes - 2)):
        over(*part, lambda p: wait_y(0, p))
    flow_part(0)
    flow_part(1)
    flow_part(2)
    over(0, planes, lambda p: wait_y(3, p))
    flow_part(3)
    halo = send_halos(4)
    lamb(X3, A3, B3, S)
    project(1)
    issue(1, 0.0, 0.1)
    settle(label, label_in, l_send, l_recv)
    place_of(label_in, place)
    settle(send.at[0], recv.at[0], a_send.at[0], a_recv.at[0])
    add_up(recv.at[0], place, forcing1)
    finish_wave(0, waves)
    wave_force(curs[1], forcing1, 0)
    waves = send_faces(1, curs[1])
    issue(1, 0.1, 0.4)
    main(1, True)
    finish_wave(1, waves)
    waves = send_faces(2, curs[2])
    arrive(halo)
    flow_part(4)
    halo = send_halos(5)
    issue(1, 0.4, 0.7)
    main(2, True)
    finish_wave(2, waves)
    waves = send_faces(3, curs[3])
    issue(1, 0.7, 1.0)
    main(3, False)
    arrive(halo)
    flow_part(5)
    for s in range(3 * STEPS):
        def drained(p, s=s):
            for c in y_copies(s, p):
                c.wait_send()
        over(0, X[s].shape[1] - 2, drained)
    drain(label, label_in, l_send, l_recv)
    drain(send.at[0], recv.at[0], a_send.at[0], a_recv.at[0])
    settle(send.at[1], recv.at[1], a_send.at[1], a_recv.at[1])
    add_up(recv.at[1], place, forcing_out)
    finish_wave(3, waves)
    wave_force(curs[4], forcing_out, 0)
    waves = send_faces(4, curs[4])
    main(4, True)
    finish_wave(4, waves)
    waves = send_faces(5, curs[5])
    main(5, True)
    drain(send.at[1], recv.at[1], a_send.at[1], a_recv.at[1])
    finish_wave(5, waves)
    for c in pending:
        c.wait_send()


def put_out(*values):
    count = len(values)

    def body(*refs):
        copies = [
            pltpu.make_async_copy(refs[i], refs[count + i], refs[2 * count].at[i])
            for i in range(count)
        ]
        for c in copies:
            c.start()
        for c in copies:
            c.wait()

    return pl.pallas_call(
        body,
        out_shape=tuple(jax.ShapeDtypeStruct(v.shape, v.dtype) for v in values),
        in_specs=[pl.BlockSpec(memory_space=pltpu.VMEM)] * count,
        out_specs=tuple([pl.BlockSpec(memory_space=pl.ANY)] * count),
        scratch_shapes=[pltpu.SemaphoreType.DMA((count,))],
        name="put_out",
    )(*[pltpu.with_memory_space_constraint(v, pltpu.VMEM) for v in values])


def local(
    density, velocity, pressure, wave_state, tables, margin_element, margin_block, margin_table
):
    flows, groups = lax.axis_size("flow"), lax.axis_size("group")
    devices = flows * groups
    planes, rows, columns = density.shape
    n, lanes = wave_state.shape[1], wave_state.shape[-1]
    table_count, depth, nodes = tables.shape
    blocks = density.size // depth
    lines = devices * 2 * CAP
    half = 3 * nodes // 2
    cols = 2 * table_count * blocks
    stages = 3 * STEPS
    side = 8
    widths = (8, 6, 4, 2, 2, 2)
    any_spec = pl.BlockSpec(memory_space=pltpu.HBM)
    vmem = pl.BlockSpec(memory_space=pltpu.VMEM)
    V = pltpu.VMEM
    DMA = pltpu.SemaphoreType.DMA
    wave_shape = wave_state.shape

    def body(*refs):
        all_kernel((flows, groups, lanes), *refs)

    fields, wave, forcing = pl.pallas_call(
        body,
        out_shape=(
            V((5, planes, rows, columns), F32),
            V(wave_shape, F32),
            V((3 * n, n, n, lanes), F32),
        ),
        in_specs=[any_spec] * 5 + [vmem] * 3,
        out_specs=(vmem, vmem, vmem),
        scratch_shapes=[
            V((planes, rows, columns), F32), V((3, planes, rows, columns), F32),
            V((planes, rows, columns), F32), V(wave_shape, F32), V(tables.shape, F32),
            V(tables.shape, BF16), V(tables.shape, BF16),
            *[V((5, planes + w, rows, columns), F32) for w in widths],
            *[V((5, planes + w - 2, side, columns), F32) for w in widths],
            *[V((5, planes + w - 2, side, columns), F32) for w in widths],
            V((3, planes, columns // 128, rows, 128), F32),
            V((lines, cols), BF16), V((devices, 1, lanes), jnp.int32), V((devices, 1, lanes), jnp.int32),
            V((lines, 2 * lanes), BF16),
            V((cols, half), BF16), V((cols, half), BF16),
            V((STEPS, lines, half), F32), V((STEPS, lines, half), F32),
            V((3 * n, n, n, lanes), F32),
            V((n, n, n, lanes), F32), V((2, n, n, lanes), F32), V((n, n, lanes), F32),
            V((5,) + wave_shape, F32),
            V((stages, 2, n, n, lanes), F32), V((stages, 2, n, n, lanes), F32),
            DMA((5,)), DMA((stages, 4)), DMA((stages, 4)),
            DMA((stages, 2, planes + 6)), DMA((stages, 2, planes + 6)),
            DMA((stages, 2)), DMA((stages, 2)), DMA(()), DMA(()),
            DMA((STEPS,)), DMA((STEPS,)),
        ],
        compiler_params=pltpu.CompilerParams(
            collective_id=0, has_side_effects=True, vmem_limit_bytes=58000 * 1024
        ),
        name="march",
    )(*[pltpu.with_memory_space_constraint(v, pltpu.HBM) for v in (density, velocity, pressure, wave_state, tables)], margin_element, margin_block, margin_table)
    fields, wave, forcing = put_out(fields, wave, forcing)
    return fields, wave, forcing.reshape((3, n, n, n, lanes))


def solution(mesh):
    in_specs = (
        P("flow", "group", None),
        P(None, "flow", "group", None),
        P("flow", "group", None),
        P(None, None, None, None, ("flow", "group")),
        P(),
        P(("flow", "group"), None),
        P(("flow", "group"), None),
        P(("flow", "group"), None),
    )
    out_specs = (
        P(None, "flow", "group", None),
        P(None, None, None, None, ("flow", "group")),
        P(None, None, None, None, ("flow", "group")),
    )
    return jax.shard_map(local, mesh=mesh, in_specs=in_specs, out_specs=out_specs, check_vma=False)
```

profile of v0, /device:TPU:0, one launch (start us, length us, event | category | flops | bytes accessed | tf_op | source)
XLA Modules:
  0.0 74.1 jit_solution(4620521929052430719)
XLA Ops:
  0.6 72.1 %march.1 = (f32[5,4,16,256]{3,2,1,0:T(8,128)S(1)}, f32[4,8,8,8,128]{4,3,2,1,0:T(8,128)S(1)}, f32[24,8,8,128]{3,2,1,0:T(8,128)S(1)}) custom-call(f32[4,16,256]{2,1,0:T(8,128)} %refs_0_.1, f32[3,4,16,256]{3,2,1,0:T(8,128)} %refs_1_.1, f32[4,16,256]{2,1,0:T(8,128)} %refs_2_.1, f32[4,8,8,8,128]{4,3,2,1,0:T(8,128)} %refs_3_.1, f32[4,512,512]{2,1,0:T(8,128)} %refs_4_.1, ...), custom_call_target="tpu_custom_call" | custom-call | tf_op jit(solution)/shard_map/march/pallas_call | solution.py:741
  72.8 1.4 %put_out.1 = (f32[5,4,16,256]{3,2,1,0:T(8,128)}, f32[4,8,8,8,128]{4,3,2,1,0:T(8,128)}, f32[24,8,8,128]{3,2,1,0:T(8,128)}) custom-call(f32[5,4,16,256]{3,2,1,0:T(8,128)S(1)} %get-tuple-element.9.refs_0_, f32[4,8,8,8,128]{4,3,2,1,0:T(8,128)S(1)} %get-tuple-element.10.refs_1_, f32[24,8,8,128]{3,2,1,0:T(8,128)S(1)} %get-tuple-element.11.refs_2_), custom_call_target="tpu_custom_call" | custom-call | tf_op jit(solution)/shard_map/put_out/pallas_call | solution.py:707
where the time goes:
time: 74.3 us; the launch traced here: 74.1 us
  Pallas kernels  73.5 us (99%)
    pallas_call x1, Pallas kernels, local(): pl.pallas_call(body, out_shape=(V((5, planes, rows, columns), F32), V(wav...  72.1 us

commit v1 on v0

--- a/solution.py
+++ b/solution.py
@@ -507,7 +507,7 @@
             device_id=at(peer), device_id_type=pl.DeviceIdType.MESH,
         )
 
-    stride = 11 if np.gcd(11, devices) == 1 else 1
+    stride = 5 if np.gcd(5, devices) == 1 else 1
 
     def exchange(src, dst, ssem, rsem, begin, end):
         def body(k, _):
@@ -537,7 +537,7 @@
         c.wait()
 
     deep = 4
-    assert planes >= deep
+    assert planes == deep and flows % 2 == 0
 
     def conserve(p, _):
         r = den[p]
@@ -556,10 +556,47 @@
         slice(deep + planes - 1, deep + planes), slice(deep - 1, deep),
     )
     over(deep - 1, deep - 1 + planes, lambda p: send_y(0, p))
-    far = send_x(
-        0, 2, slice(deep + 1, 2 * deep), slice(deep + planes + 1, 2 * deep + planes),
-        slice(planes, deep + planes - 1), slice(0, deep - 1),
-    )
+    odd = f % 2
+    partner = ((f + 1 - 2 * odd) % flows, g)
+    beyond = ((f + 2 - 4 * odd + flows) % flows, g)
+    pick_by = lambda even_value, odd_value: even_value + odd * (odd_value - even_value)
+
+    def x_plane(src, dst, i, device):
+        return pltpu.make_async_remote_copy(
+            src_ref=X0.at[:, pl.ds(src, 1)], dst_ref=X0.at[:, pl.ds(dst, 1)],
+            send_sem=x_send.at[0, i], recv_sem=x_recv.at[0, i],
+            device_id=device, device_id_type=pl.DeviceIdType.MESH,
+        )
+
+    def direct(d):
+        return x_plane(
+            pick_by(deep + planes - d, deep + d - 1), pick_by(deep - d, deep + planes + d - 1),
+            d, partner,
+        )
+
+    def onward(d):
+        return x_plane(
+            pick_by(deep + planes + d - 1, deep - d),
+            pick_by(deep - planes + d - 1, deep + 2 * planes - d), deep + d, beyond,
+        )
+
+    def near_of(side):
+        return pltpu.make_async_remote_copy(
+            src_ref=X0.at[:, 0:1], dst_ref=X0.at[:, 0:1],
+            send_sem=x_send.at[0, side], recv_sem=x_recv.at[0, side],
+            device_id=partner, device_id_type=pl.DeviceIdType.MESH,
+        )
+
+    for d in range(2, deep + 1):
+        direct(d).start()
+
+    def pass_on(d):
+        if d == 1:
+            near_of(odd).wait_recv()
+        else:
+            direct(d).wait_recv()
+        onward(d).start()
+
     loads[3].wait()
     waves = send_faces(0, wave0)
     blocks = planes * rows * columns // tables.shape[1]
@@ -627,13 +664,18 @@
         wave_faces(curs[s], curs[s + 1], FR.at[s, 0], FR.at[s, 1], lift, s % 3)
 
     main(0, False)
-    arrive(near)
+    pass_on(1)
+    near_of(1 - odd).wait_recv()
     over(deep - 1, deep - 1 + planes, lambda p: wait_y(0, p))
     mid, own = pl.ds(deep - 1, planes + 2), pl.ds(deep - 1, planes)
     lamb(X0.at[:, mid], A0.at[:, own], B0.at[:, own], S)
+    pass_on(2)
     project(0)
+    pass_on(3)
     issue(0, 0.0, 1.0)
-    arrive(far)
+    direct(deep).wait_recv()
+    for d in range(1, deep):
+        onward(d).wait_recv()
     for part in ((0, deep - 1), (deep - 1 + planes, 2 * deep + planes - 2)):
         over(*part, lambda p: send_y(0, p))
     for part in ((0, deep - 1), (deep - 1 + planes, 2 * deep + planes - 2)):
@@ -646,7 +688,7 @@
     halo = send_halos(4)
     lamb(X3, A3, B3, S)
     project(1)
-    issue(1, 0.0, 0.1)
+    issue(1, 0.0, 0.2)
     settle(label, label_in, l_send, l_recv)
     place_of(label_in, place)
     settle(send.at[0], recv.at[0], a_send.at[0], a_recv.at[0])
@@ -654,18 +696,18 @@
     finish_wave(0, waves)
     wave_force(curs[1], forcing1, 0)
     waves = send_faces(1, curs[1])
-    issue(1, 0.1, 0.4)
+    issue(1, 0.2, 0.6)
     main(1, True)
     finish_wave(1, waves)
     waves = send_faces(2, curs[2])
     arrive(halo)
     flow_part(4)
     halo = send_halos(5)
-    issue(1, 0.4, 0.7)
+    issue(1, 0.6, 0.9)
     main(2, True)
     finish_wave(2, waves)
     waves = send_faces(3, curs[3])
-    issue(1, 0.7, 1.0)
+    issue(1, 0.9, 1.0)
     main(3, False)
     arrive(halo)
     flow_part(5)
@@ -675,6 +717,9 @@
                 c.wait_send()
         over(0, X[s].shape[1] - 2, drained)
     drain(label, label_in, l_send, l_recv)
+    for d in range(1, deep):
+        direct(d + 1).wait_send()
+        onward(d).wait_send()
     drain(send.at[0], recv.at[0], a_send.at[0], a_recv.at[0])
     settle(send.at[1], recv.at[1], a_send.at[1], a_recv.at[1])
     add_up(recv.at[1], place, forcing_out)
@@ -763,7 +808,7 @@
             V((n, n, n, lanes), F32), V((2, n, n, lanes), F32), V((n, n, lanes), F32),
             V((5,) + wave_shape, F32),
             V((stages, 2, n, n, lanes), F32), V((stages, 2, n, n, lanes), F32),
-            DMA((5,)), DMA((stages, 4)), DMA((stages, 4)),
+            DMA((5,)), DMA((stages, 8)), DMA((stages, 8)),
             DMA((stages, 2, planes + 6)), DMA((stages, 2, planes + 6)),
             DMA((stages, 2)), DMA((stages, 2)), DMA(()), DMA(()),
             DMA((STEPS,)), DMA((STEPS,)),

time: 74.3 us -> 70.1 us (0.943)
  Pallas kernels: 73.5 us -> 69.3 us
    pallas_call x1, Pallas kernels: 72.1 us -> 67.9 us  [local(): pl.pallas_call(body, out_shape=(V((5, planes, rows, columns), F32), V(wav...]
where the time goes in v1:
time: 70.1 us; the launch traced here: 69.9 us
  Pallas kernels  69.3 us (99%)
    pallas_call x1, Pallas kernels, local(): pl.pallas_call(body, out_shape=(V((5, planes, rows, columns), F32), V(wav...  67.9 us

profile of v1, /device:TPU:0, one launch (start us, length us, event | category | flops | bytes accessed | tf_op | source)
XLA Modules:
  0.0 69.9 jit_solution(10056865200525937980)
XLA Ops:
  0.6 67.9 %march.1 = (f32[5,4,16,256]{3,2,1,0:T(8,128)S(1)}, f32[4,8,8,8,128]{4,3,2,1,0:T(8,128)S(1)}, f32[24,8,8,128]{3,2,1,0:T(8,128)S(1)}) custom-call(f32[4,16,256]{2,1,0:T(8,128)} %refs_0_.1, f32[3,4,16,256]{3,2,1,0:T(8,128)} %refs_1_.1, f32[4,16,256]{2,1,0:T(8,128)} %refs_2_.1, f32[4,8,8,8,128]{4,3,2,1,0:T(8,128)} %refs_3_.1, f32[4,512,512]{2,1,0:T(8,128)} %refs_4_.1, ...), custom_call_target="tpu_custom_call" | custom-call | tf_op jit(solution)/shard_map/march/pallas_call | solution.py:786
  68.5 1.4 %put_out.1 = (f32[5,4,16,256]{3,2,1,0:T(8,128)}, f32[4,8,8,8,128]{4,3,2,1,0:T(8,128)}, f32[24,8,8,128]{3,2,1,0:T(8,128)}) custom-call(f32[5,4,16,256]{3,2,1,0:T(8,128)S(1)} %get-tuple-element.9.refs_0_, f32[4,8,8,8,128]{4,3,2,1,0:T(8,128)S(1)} %get-tuple-element.10.refs_1_, f32[24,8,8,128]{3,2,1,0:T(8,128)S(1)} %get-tuple-element.11.refs_2_), custom_call_target="tpu_custom_call" | custom-call | tf_op jit(solution)/shard_map/put_out/pallas_call | solution.py:752
